TPU v7x, 32 devices: a whole 2x2x4 slice. The times are simulated.
32 devices in a mesh: row: 8 (over z, x), col: 2 (over core), dp: 2 (over y).
Axes of the slice: x: 2, y: 2, z: 4, core: 2. Of those that a mesh axis runs over, the one named last changes fastest.
Arguments:
- pixels: bfloat16 [2, 3, 256, 256], P('dp', None, 'row', 'col'), may hold values from -6 to 6
- cotangent: bfloat16 [2, 64, 64, 1024], P('dp', 'row', 'col'), may hold values from -6 to 6
- embed_weight: bfloat16 [48, 1024], replicated, may hold values from -0.875 to 0.875
- embed_bias: float32 [1024], replicated, may hold values from -4 to 4
- layer_norm_gain: float32 [1024], replicated, may hold values from 0.5 to 1.5
- qkv_weight: bfloat16 [1024, 2304], P('row', ('col', 'dp')), may hold values from -0.1875 to 0.1875
- out_weight: bfloat16 [768, 1024], P('row', ('col', 'dp')), may hold values from -0.21875 to 0.21875
- bias_table: float32 [12, 225], replicated, may hold values from -4 to 404
- rel_index: int32 [64, 64], replicated, may hold values from 0 to 224
- shifts: int32 [2, 2], P('dp'), may hold values from 1 to 7
Outputs:
- out_weight_grad: float32 [768, 1024], P('row', ('col', 'dp'))
- embed_weight_grad: float32 [48, 1024], replicated
- embed_bias_grad: float32 [1024], replicated
- norm_gain_grad: float32 [1024], replicated
- bias_table_grad: float32 [12, 225], replicated
Inputs may be any that keep to these rules, and one draw needn't show every extreme that they name: `rel_index`: each entry names one of the 225 columns of bias_table.
All inputs are finite; a program needn't handle non-finite values.
Results may differ from a plain program's by a relative error of at most 0.023.
Values may be sent and summed in bfloat16 or wider, within the bound.
A program may use at most 64 MiB of HBM per device.

v0:
```python
import jax
import jax.numpy as jnp
from jax import lax
from jax.sharding import PartitionSpec as P

WIN = 8
PATCH = 4
norm_epsilon = 1e-05


def from_behind(value, axis, steps):
    count = lax.axis_size(axis)
    pairs = [(source, (source + steps) % count) for source in range(count)]
    return lax.ppermute(value, axis, pairs)


def make_patches(pixel_block):
    images, channels, pixel_rows, pixel_cols = pixel_block.shape
    grid_rows = pixel_rows // PATCH
    grid_cols = pixel_cols // PATCH
    shaped = pixel_block.reshape(images, channels, grid_rows, PATCH, grid_cols, PATCH)
    return shaped.transpose(0, 2, 4, 1, 3, 5).reshape(
        images, grid_rows, grid_cols, channels * PATCH * PATCH
    )


def embed_cells(patches, embed_weight, embed_bias):
    return (jnp.dot(patches, embed_weight, preferred_element_type=jnp.float32) + embed_bias).astype(
        jnp.bfloat16
    )


def window_split(block):
    rows_all, cols_all, features = block.shape
    shaped = block.reshape(rows_all // WIN, WIN, cols_all // WIN, WIN, features)
    return shaped.transpose(0, 2, 1, 3, 4).reshape(-1, WIN * WIN, features)


def window_join(windows, rows_all, cols_all):
    features = windows.shape[-1]
    shaped = windows.reshape(rows_all // WIN, cols_all // WIN, WIN, WIN, features)
    return shaped.transpose(0, 2, 1, 3, 4).reshape(rows_all, cols_all, features)


def splice_after(own_block, borrowed, offsets, along_dim):
    length = own_block.shape[along_dim]

    def single(own_item, borrowed_item, offset):
        joined = jnp.concatenate([own_item, borrowed_item], along_dim - 1)
        return lax.dynamic_slice_in_dim(joined, offset, length, along_dim - 1)

    return jax.vmap(single)(own_block, borrowed, offsets)


def splice_before(own_block, borrowed, offsets, along_dim):
    length = own_block.shape[along_dim]
    margin = borrowed.shape[along_dim]

    def single(own_item, borrowed_item, offset):
        joined = jnp.concatenate([borrowed_item, own_item], along_dim - 1)
        return lax.dynamic_slice_in_dim(joined, margin - offset, length, along_dim - 1)

    return jax.vmap(single)(own_block, borrowed, offsets)


def attend_forward(cell_windows, labels, layer_norm_gain, qkv_full, bias_full):
    window_count, cell_count, features = cell_windows.shape
    head_count = bias_full.shape[0]
    inner_width = qkv_full.shape[1] // 3
    head_size = inner_width // head_count
    score_scale = head_size ** (-0.5)
    flat_rows = cell_windows.reshape(-1, features).astype(jnp.float32)
    average = jnp.mean(flat_rows, axis=-1, keepdims=True)
    centered_input = flat_rows - average
    inverse_deviation = lax.rsqrt(
        jnp.mean(centered_input * centered_input, axis=-1, keepdims=True) + norm_epsilon
    )
    standardized_rows = centered_input * inverse_deviation
    normalized_rows = (standardized_rows * layer_norm_gain).astype(jnp.bfloat16)
    projected = jnp.dot(normalized_rows, qkv_full, preferred_element_type=jnp.float32).astype(
        jnp.bfloat16
    )
    head_shape = (window_count, cell_count, head_count, head_size)
    query_rows = projected[:, :inner_width].reshape(head_shape)
    key_vectors = projected[:, inner_width : 2 * inner_width].reshape(head_shape)
    value_rows = projected[:, 2 * inner_width :].reshape(head_shape)
    scores = (
        jnp.einsum("wmhd,wnhd->whmn", query_rows, key_vectors, preferred_element_type=jnp.float32)
        * score_scale
        + bias_full[None]
    )
    same_region = labels[:, None, :, None] == labels[:, None, None, :]
    scores = jnp.where(same_region, scores, -1e30)
    row_peak = jnp.max(scores, axis=-1, keepdims=True)
    exp_scores = jnp.exp(scores - row_peak)
    attention_weights = exp_scores / jnp.sum(exp_scores, axis=-1, keepdims=True)
    reduced_probability = attention_weights.astype(jnp.bfloat16)
    attended = jnp.einsum(
        "whmn,wnhd->wmhd", reduced_probability, value_rows, preferred_element_type=jnp.float32
    ).astype(jnp.bfloat16)
    stored_residuals = (
        standardized_rows,
        inverse_deviation,
        query_rows,
        key_vectors,
        value_rows,
        attention_weights,
        reduced_probability,
    )
    return (stored_residuals, attended.reshape(-1, inner_width))


def attend_backward(stored_residuals, d_attended, layer_norm_gain, qkv_full):
    (
        standardized_rows,
        inverse_deviation,
        query_rows,
        key_vectors,
        value_rows,
        attention_weights,
        reduced_probability,
    ) = stored_residuals
    head_shape = query_rows.shape
    score_scale = head_shape[3] ** (-0.5)
    total_row_count = standardized_rows.shape[0]
    inner_width = head_shape[2] * head_shape[3]
    d_heads = d_attended.reshape(head_shape)
    d_prob = jnp.einsum("wmhd,wnhd->whmn", d_heads, value_rows, preferred_element_type=jnp.float32)
    d_values = jnp.einsum(
        "whmn,wmhd->wnhd", reduced_probability, d_heads, preferred_element_type=jnp.float32
    ).astype(jnp.bfloat16)
    d_scores = attention_weights * (
        d_prob - jnp.sum(attention_weights * d_prob, axis=-1, keepdims=True)
    )
    table_part = jnp.sum(d_scores, axis=0)
    d_low = d_scores.astype(jnp.bfloat16)
    d_queries = (
        jnp.einsum("whmn,wnhd->wmhd", d_low, key_vectors, preferred_element_type=jnp.float32)
        * score_scale
    ).astype(jnp.bfloat16)
    d_keys = (
        jnp.einsum("whmn,wmhd->wnhd", d_low, query_rows, preferred_element_type=jnp.float32)
        * score_scale
    ).astype(jnp.bfloat16)
    d_projected = jnp.concatenate(
        [
            d_queries.reshape(total_row_count, inner_width),
            d_keys.reshape(total_row_count, inner_width),
            d_values.reshape(total_row_count, inner_width),
        ],
        axis=1,
    )
    normalized_gradient = lax.dot_general(
        d_projected, qkv_full, (((1,), (1,)), ((), ())), preferred_element_type=jnp.float32
    )
    gain_contribution = jnp.sum(normalized_gradient * standardized_rows, axis=0)
    scaled_rows = normalized_gradient * layer_norm_gain
    branch_gradient = inverse_deviation * (
        scaled_rows
        - jnp.mean(scaled_rows, axis=-1, keepdims=True)
        - standardized_rows * jnp.mean(scaled_rows * standardized_rows, axis=-1, keepdims=True)
    )
    return (branch_gradient.astype(jnp.bfloat16), gain_contribution, table_part)


def on_device(
    pixels,
    cotangent,
    embed_weight,
    embed_bias,
    layer_norm_gain,
    qkv_weight,
    out_weight,
    bias_table,
    rel_index,
    shifts,
):
    images, rows_dev, cols_dev, features = cotangent.shape
    head_count = bias_table.shape[0]
    grid_rows = rows_dev * lax.axis_size("row")
    grid_cols = cols_dev * lax.axis_size("col")
    row_shift = shifts[:, 0]
    col_shift = shifts[:, 1]
    qkv_rowwise = lax.all_gather(qkv_weight, "row", axis=0, tiled=True)
    qkv_full, out_columns = (
        lax.all_gather(qkv_rowwise, ("col", "dp"), axis=1, tiled=True),
        lax.all_gather(out_weight, ("col", "dp"), axis=1, tiled=True),
    )
    patches = make_patches(pixels)
    tokens = embed_cells(patches, embed_weight, embed_bias)
    below = from_behind((tokens, cotangent), "row", -1)
    shifted = splice_after(tokens, below[0], row_shift, 1)
    shifted_cot = splice_after(cotangent, below[1], row_shift, 1)
    beside = from_behind((shifted[:, :, :WIN], shifted_cot[:, :, :WIN]), "col", -1)
    shifted = splice_after(shifted, beside[0], col_shift, 2)
    shifted_cot = splice_after(shifted_cot, beside[1], col_shift, 2)
    row_ids = lax.axis_index("row") * rows_dev + jnp.arange(rows_dev, dtype=jnp.int32)
    col_ids = lax.axis_index("col") * cols_dev + jnp.arange(cols_dev, dtype=jnp.int32)
    row_part = (row_ids[None, :] >= grid_rows - row_shift[:, None]).astype(jnp.int32)
    col_part = (col_ids[None, :] >= grid_cols - col_shift[:, None]).astype(jnp.int32)
    region = 2 * row_part[:, :, None] + col_part[:, None, :]
    labels = window_split(region.reshape(images * rows_dev, cols_dev, 1))[:, :, 0]
    cell_windows = window_split(shifted.reshape(images * rows_dev, cols_dev, features))
    cot_flat = window_split(shifted_cot.reshape(images * rows_dev, cols_dev, features)).reshape(
        -1, features
    )
    selector = (
        rel_index.reshape(-1)[:, None] == jnp.arange(bias_table.shape[1], dtype=jnp.int32)[None, :]
    ).astype(jnp.float32)
    bias_full = jnp.dot(selector, bias_table.T, precision=lax.Precision.HIGHEST).T.reshape(
        head_count, WIN * WIN, WIN * WIN
    )
    stored_residuals, attended = attend_forward(
        cell_windows, labels, layer_norm_gain, qkv_full, bias_full
    )
    d_attended = lax.dot_general(
        cot_flat,
        lax.all_gather(out_columns, "row", axis=0, tiled=True),
        (((1,), (1,)), ((), ())),
        preferred_element_type=jnp.float32,
    ).astype(jnp.bfloat16)
    partial_rows = lax.psum_scatter(
        lax.dot_general(
            attended, cot_flat, (((0,), (0,)), ((), ())), preferred_element_type=jnp.float32
        ),
        "row",
        scatter_dimension=0,
        tiled=True,
    )
    out_weight_grad = lax.psum_scatter(partial_rows, ("col", "dp"), scatter_dimension=1, tiled=True)
    d_rows, gain_contribution, table_part = attend_backward(
        stored_residuals, d_attended, layer_norm_gain, qkv_full
    )
    branch_gradient = window_join(
        d_rows.reshape(-1, WIN * WIN, features), images * rows_dev, cols_dev
    ).reshape(images, rows_dev, cols_dev, features)
    patch_rows = patches.reshape(-1, patches.shape[-1])
    cot_rows = cotangent.reshape(-1, features)
    contract = (((0,), (0,)), ((), ()))
    behind = from_behind(branch_gradient[:, :, cols_dev - WIN :], "col", 1)
    d_back = splice_before(branch_gradient, behind, col_shift, 2)
    above = from_behind(d_back, "row", 1)
    d_back = splice_before(d_back, above, row_shift, 1)
    back_rows = d_back.reshape(-1, features)
    embed_grad = lax.dot_general(
        patch_rows, cot_rows, contract, preferred_element_type=jnp.float32
    ) + lax.dot_general(patch_rows, back_rows, contract, preferred_element_type=jnp.float32)
    bias_grad = jnp.sum(cot_rows, axis=0, dtype=jnp.float32) + jnp.sum(
        back_rows, axis=0, dtype=jnp.float32
    )
    table_grad = jnp.dot(
        table_part.reshape(head_count, -1), selector, precision=lax.Precision.HIGHEST
    )
    totals = lax.psum((embed_grad, bias_grad, gain_contribution, table_grad), ("row", "col", "dp"))
    return (out_weight_grad, totals[0], totals[1], totals[2], totals[3])


def solution(mesh):
    return jax.shard_map(
        on_device,
        mesh=mesh,
        in_specs=(
            P("dp", None, "row", "col"),
            P("dp", "row", "col", None),
            P(),
            P(),
            P(),
            P("row", ("col", "dp")),
            P("row", ("col", "dp")),
            P(),
            P(),
            P("dp", None),
        ),
        out_specs=(P("row", ("col", "dp")), P(), P(), P(), P()),
        check_vma=False,
    )
```

profile of v0, /device:TPU:0, one launch (start us, length us, event | category | flops | bytes accessed | tf_op | source)
XLA Modules:
  0.0 390.5 jit_solution(13253919688802146951)
XLA Ops:
  8.0 45.2 %all-gather.4.cloned.1.call-done = bf16[1024,576]{0,1:T(8,128)(2,1)} async-done(((bf16[128,576]{0,1:T(8,128)(2,1)}), bf16[1024,576]{0,1:T(8,128)(2,1)}) %all-gather.4.cloned.1.call-update) | async-done | bytes 1179664 | tf_op jit(solution)/shard_map/all_gather | solution.py:184
  55.4 2.4 reshape.177
  60.0 12.5 %all_gather.14 = bf16[96,1024]{1,0:T(8,128)(2,1)} all-gather(bf16[96,256]{1,0:T(8,128)(2,1)S(1)} %copy-done.13), channel_id=1, replica_groups=mesh['row'=8,'col'=2,'dp'=2] {'col','dp'}, dimensions={1}, use_global_device_ids=true | all-gather | bytes 245760 | tf_op jit(solution)/shard_map/all_gather | solution.py:187
  76.8 2.6 convolution_bitcast_fusion
  86.7 7.0 %all-gather.6.cloned.1.call-done = bf16[1024,2304]{0,1:T(8,128)(2,1)} async-done(((bf16[1024,576]{0,1:T(8,128)(2,1)}), bf16[1024,2304]{0,1:T(8,128)(2,1)}) %all-gather.6.cloned.1.call-update) | async-done | bytes 4718608 | tf_op jit(solution)/shard_map/all_gather | solution.py:186
  93.7 3.8 convolution_convert_fusion
  99.9 2.5 reshape.366
  109.0 3.8 fusion.7
  112.7 2.7 copy.168
  115.4 2.5 reshape.182
  117.9 3.4 fusion.46
  121.5 17.9 %all-gather.8.cloned.1.call-done = bf16[768,1024]{1,0:T(8,128)(2,1)} async-done(((bf16[96,1024]{1,0:T(8,128)(2,1)}), bf16[768,1024]{1,0:T(8,128)(2,1)}) %all-gather.8.cloned.1.call-update) | async-done | bytes 1572880 | tf_op jit(solution)/shard_map/all_gather | solution.py:218
  139.4 3.0 convolution_convert_fusion.3
  142.4 2.4 reshape.369
  144.8 2.5 copy.182
  147.3 2.8 multiply_reduce_fusion
  156.0 2.5 reshape.185
  162.8 3.5 fusion.8
  169.3 4.2 %multiply_reduce_fusion.1 = (f32[1024]{0:T(1024)S(1)}, f32[256]{0:T(256)S(1)}, f32[256]{0:T(256)S(1)}, f32[256,1024]{1,0:T(8,128)S(1)}) fusion(f32[1,4,8,8,1024]{4,3,2,1,0:T(8,128)S(1)} %copy.156, f32[256]{0:T(256)S(1)} %rsqrt.12, f32[256]{0:T(256)S(1)} %div.23, f32[1024]{0:T(1024)S(1)} %copy-done.15, bf16[1024,2304]{0,1:T(8,128)(2,1)} %all-gather.6.cloned.1.call-done, ...), kind=kOutput, calls=%fused_computation.41 | convolution fusion | flops 1213594112 | bytes 8007680 | tf_op jit(solution)/shard_map/dot_general | solution.py:153
  177.6 15.2 %collective-permute-done.5 = bf16[1,8,32,1024]{3,2,1,0:T(8,128)(2,1)S(1)} collective-permute-done((bf16[1,8,32,1024]{3,2,1,0:T(8,128)(2,1)S(1)}, bf16[1,8,32,1024]{3,2,1,0:T(8,128)(2,1)S(1)}, u32[]{:S(2)}, u32[]{:S(2)}) %collective-permute-start.5) | collective-permute-done | bytes 524320 | tf_op jit(solution)/shard_map/ppermute | solution.py:14
  194.0 33.6 %reduce-scatter.3.cloned.1.call-done = f32[96,1024]{1,0:T(8,128)} async-done(((f32[768,1024]{1,0:T(8,128)}), f32[96,1024]{1,0:T(8,128)}) %reduce-scatter.3.cloned.1.call-update) | async-done | bytes 393232 | tf_op jit(solution)/shard_map/reduce_scatter | solution.py:222
  229.5 40.2 %all-reduce.2 = (f32[1024]{0:T(1024)}, f32[1024]{0:T(1024)}, f32[12,225]{1,0:T(8,128)}) all-reduce(f32[1024]{0:T(1024)S(1)} %add.134, f32[1024]{0:T(1024)S(1)} %get-tuple-element.71, f32[12,225]{1,0:T(8,128)S(1)} %fusion.1), channel_id=1, replica_groups=mesh['row'=8,'col'=2,'dp'=2] {'row','col','dp'}, use_global_device_ids=true, to_apply=%region_12.13 | all-reduce | flops 4748 | bytes 37984 | tf_op jit(solution)/shard_map/psum | solution.py:254
  269.7 87.6 %all-reduce.5.cloned.1.call-done = f32[48,1024]{1,0:T(8,128)} async-done(((f32[48,1024]{1,0:T(8,128)}), f32[48,1024]{1,0:T(8,128)}) %all-reduce.5.cloned.1.call-update) | async-done | bytes 196624 | tf_op jit(solution)/shard_map/psum | solution.py:254
  357.4 24.7 %reduce-scatter.5.cloned.1.call-done = f32[96,256]{1,0:T(8,128)} async-done(((f32[96,1024]{1,0:T(8,128)}), f32[96,256]{1,0:T(8,128)}) %reduce-scatter.5.cloned.1.call-update) | async-done | bytes 98320 | tf_op jit(solution)/shard_map/reduce_scatter | solution.py:230
  (121 shorter events, 39.7 us)
Async XLA Ops:
  7.2 51.3 %copy-start = (bf16[48,1024]{1,0:T(8,128)(2,1)S(1)}, bf16[48,1024]{1,0:T(8,128)(2,1)}, u32[]{:S(2)}) copy-start(bf16[48,1024]{1,0:T(8,128)(2,1)} %param.12) | copy-start | bytes 294916
  7.2 51.3 %copy-start.18 = (f32[1024]{0:T(1024)S(1)}, f32[1024]{0:T(1024)}, u32[]{:S(2)}) copy-start(f32[1024]{0:T(1024)} %param.13) | copy-start | bytes 12292
  7.2 45.9 %all-gather.4.cloned.1.call-start = ((), (), s32[]{:S(2)}) async-start(), calls=%async_computation.2 | async-start | bytes 1327104 | tf_op jit(solution)/shard_map/all_gather | solution.py:184
  7.9 85.8 %all-gather.6.cloned.1.call-start = ((), (), s32[]{:S(2)}) async-start(), calls=%async_computation.3 | async-start | bytes 5898240 | tf_op jit(solution)/shard_map/all_gather | solution.py:186
  53.1 6.9 %copy-start.13 = (bf16[96,256]{1,0:T(8,128)(2,1)S(1)}, bf16[96,256]{1,0:T(8,128)(2,1)}, u32[]{:S(2)}) copy-start(bf16[96,256]{1,0:T(8,128)(2,1)} %param.16) | copy-start | bytes 147460
  53.2 19.5 %copy-start.19 = (s32[1,2]{1,0:T(1,128)S(1)}, s32[1,2]{1,0:T(1,128)}, u32[]{:S(2)}) copy-start(s32[1,2]{1,0:T(1,128)} %param.19) | copy-start | bytes 28
  53.2 22.8 %copy-start.14 = (s32[64,64]{1,0:T(8,128)S(1)}, s32[64,64]{1,0:T(8,128)}, u32[]{:S(2)}) copy-start(s32[64,64]{1,0:T(8,128)} %param.18) | copy-start | bytes 49156
  53.2 23.6 %copy-start.20 = (f32[12,225]{1,0:T(8,128)S(1)}, f32[12,225]{1,0:T(8,128)}, u32[]{:S(2)}) copy-start(f32[12,225]{1,0:T(8,128)} %param.17) | copy-start | bytes 32404
  53.2 86.2 %all-gather.8.cloned.1.call-start = ((), (), s32[]{:S(2)}) async-start(), calls=%async_computation.6 | async-start | bytes 1769472 | tf_op jit(solution)/shard_map/all_gather | solution.py:218
  53.2 29.6 %collective-permute-start.2 = (bf16[1,8,32,1024]{3,2,1,0:T(8,128)(2,1)}, bf16[1,8,32,1024]{3,2,1,0:T(8,128)(2,1)S(1)}, u32[]{:S(2)}, u32[]{:S(2)}) collective-permute-start(bf16[1,8,32,1024]{3,2,1,0:T(8,128)(2,1)} %param.11), channel_id=1, source_target_pairs={{0,28},{4,0},{8,4},{12,8},{16,12},{20,16},{24,20},{28,24},{1,29},{... | collective-permute-start | bytes 1572872 | tf_op jit(solution)/shard_map/ppermute | solution.py:14
  58.5 20.9 %copy-start.8 = (bf16[1,8,32,3,4,4]{2,1,5,4,3,0:T(8,128)(2,1)}, bf16[1,8,32,3,4,4]{2,1,5,4,3,0:T(8,128)(2,1)S(1)}, u32[]{:S(2)}) copy-start(bf16[1,8,32,3,4,4]{2,1,5,4,3,0:T(8,128)(2,1)S(1)} %copy.154) | copy-start | bytes 73732
  58.8 20.5 %collective-permute-start = (bf16[1,8,32,1024]{3,2,1,0:T(8,128)(2,1)S(1)}, bf16[1,8,32,1024]{3,2,1,0:T(8,128)(2,1)S(1)}, u32[]{:S(2)}, u32[]{:S(2)}) collective-permute-start(bf16[1,8,32,1024]{3,2,1,0:T(8,128)(2,1)S(1)} %fusion.11), channel_id=1, source_target_pairs={{0,28},{4,0},{8,4},{12,8},{16,12},{20,16},{24,20},{28,24},{1,29},{... | collective-permute-start | bytes 1572872 | tf_op jit(solution)/shard_map/ppermute | solution.py:14
  72.6 155.0 %reduce-scatter.3.cloned.1.call-start = ((), (), s32[]{:S(2)}) async-start(), calls=%async_computation.4 | async-start | bytes 3538944 | tf_op jit(solution)/shard_map/reduce_scatter | solution.py:222
  76.1 3.3 copy-start.16
  79.4 3.5 copy-start.5
  79.6 4.0 %collective-permute-start.1 = (bf16[1,8,8,1024]{3,2,1,0:T(8,128)(2,1)S(1)}, bf16[1,8,8,1024]{3,2,1,0:T(8,128)(2,1)S(1)}, u32[]{:S(2)}, u32[]{:S(2)}) collective-permute-start(bf16[1,8,8,1024]{3,2,1,0:T(8,128)(2,1)S(1)} %slice.150), channel_id=1, source_target_pairs={{0,2},{2,0},{1,3},{3,1},{4,6},{6,4},{5,7},{7,5},{8,10},{10,8},{9,1... | collective-permute-start | bytes 393224 | tf_op jit(solution)/shard_map/ppermute | solution.py:14
  83.1 1.5 collective-permute-start.3
  121.3 236.1 %all-reduce.5.cloned.1.call-start = ((), (), s32[]{:S(2)}) async-start(), calls=%async_computation.7 | async-start | bytes 393216 | tf_op jit(solution)/shard_map/psum | solution.py:254
  153.8 4.8 %copy-start.2 = (bf16[4,12,64,64]{2,3,1,0:T(8,128)(2,1)S(1)}, bf16[4,12,64,64]{2,3,1,0:T(8,128)(2,1)}, u32[]{:S(2)}) copy-start(bf16[4,12,64,64]{2,3,1,0:T(8,128)(2,1)} %copy-done.1) | copy-start | bytes 1179652
  174.0 1.4 collective-permute-start.4
  175.6 17.2 %collective-permute-start.5 = (bf16[1,8,32,1024]{3,2,1,0:T(8,128)(2,1)S(1)}, bf16[1,8,32,1024]{3,2,1,0:T(8,128)(2,1)S(1)}, u32[]{:S(2)}, u32[]{:S(2)}) collective-permute-start(bf16[1,8,32,1024]{3,2,1,0:T(8,128)(2,1)S(1)} %fusion.25), channel_id=1, source_target_pairs={{0,4},{4,8},{8,12},{12,16},{16,20},{20,24},{24,28},{28,0},{1,5},{5... | collective-permute-start | bytes 1572872 | tf_op jit(solution)/shard_map/ppermute | solution.py:14
  192.7 35.0 %copy-start.6 = (f32[12,64,64]{1,2,0:T(8,128)S(1)}, f32[12,64,64]{1,2,0:T(8,128)}, u32[]{:S(2)}) copy-start(f32[12,64,64]{1,2,0:T(8,128)} %get-tuple-element.81) | copy-start | bytes 589828
  193.0 35.0 %copy-start.17 = (s32[4096]{0:T(1024)S(1)}, s32[4096]{0:T(1024)}, u32[]{:S(2)}) copy-start(s32[4096]{0:T(1024)} %copy-done.16) | copy-start | bytes 49156
  193.9 188.1 %reduce-scatter.5.cloned.1.call-start = ((), (), s32[]{:S(2)}) async-start(), calls=%async_computation.5 | async-start | bytes 491520 | tf_op jit(solution)/shard_map/reduce_scatter | solution.py:230
  (9 other events, 20.3 us)
Sparse Core Ops, SparseCore 0:
  10.0 43.0 all-gather.3
  54.7 38.9 all-gather.5
  95.9 43.4 all-gather.7
  142.9 84.6 reduce-scatter.2
  233.6 123.7 all-reduce.4
  360.3 21.7 reduce-scatter.4
where the time goes:
time: 391 us
  waiting for transfers between devices  233 us (60%)
  blocking collectives  52.7 us (13%)
  local copies, waits for them, and re-layouts  38.4 us (10%)
  matrix products  34.1 us (9%)
  between operations  22.4 us (6%)
  other arithmetic  5.59 us (1%)
  starting transfers between devices  4.81 us (1%)
    psum x1, waiting for transfers between devices, on_device(): lax.psum((embed_grad, bias_grad, gain_contribution, table_grad), ('row',...  87.6 us
    all_gather x1, waiting for transfers between devices, on_device(): qkv_rowwise = lax.all_gather(qkv_weight, 'row', axis=0, tiled=True)  45.2 us
    psum x1, blocking collectives, on_device(): lax.psum((embed_grad, bias_grad, gain_contribution, table_grad), ('row',...  40.2 us
    reduce_scatter x1, waiting for transfers between devices, on_device(): lax.psum_scatter(lax.dot_general(attended, cot_flat, (((0,), (0,)), ((),...  33.6 us
    reduce_scatter x1, waiting for transfers between devices, on_device(): lax.psum_scatter(partial_rows, ('col', 'dp'), scatter_dimension=1, tiled=...  24.7 us
    all_gather x1, waiting for transfers between devices, on_device(): lax.all_gather(out_columns, 'row', axis=0, tiled=True)  17.9 us
    ppermute x6, waiting for transfers between devices, from_behind(): return lax.ppermute(value, axis, pairs)  15.7 us
    all_gather x1, blocking collectives, on_device(): lax.all_gather(out_weight, ('col', 'dp'), axis=1, tiled=True)  12.5 us
  transfers between devices with their start and end apart: 12, of which 8 were waited for; matrix products, arithmetic and copies ran while one was open for 19% of the time, Pallas kernels for 0%

commit v1 on v0

--- a/solution.py
+++ b/solution.py
@@ -251,7 +251,9 @@
     table_grad = jnp.dot(
         table_part.reshape(head_count, -1), selector, precision=lax.Precision.HIGHEST
     )
-    totals = lax.psum((embed_grad, bias_grad, gain_contribution, table_grad), ("row", "col", "dp"))
+    totals = lax.psum(
+        lax.psum((embed_grad, bias_grad, gain_contribution, table_grad), "row"), ("col", "dp")
+    )
     return (out_weight_grad, totals[0], totals[1], totals[2], totals[3])
 
 

time: 391 us -> 414 us (1.059)
  waiting for transfers between devices: 233 us -> 256 us
  local copies, waits for them, and re-layouts: 38.4 us -> 26.7 us
  blocking collectives: 52.7 us -> 62.1 us
    reduce_scatter x1, waiting for transfers between devices: 33.6 us -> 76.8 us  [on_device(): lax.psum_scatter(lax.dot_general(attended, cot_flat, (((0,), (0,)), ((),...]
    all_gather x1, waiting for transfers between devices: 7.04 us -> 31.3 us  [on_device(): lax.all_gather(qkv_rowwise, ('col', 'dp'), axis=1, tiled=True)]
    psum x1 -> x2, waiting for transfers between devices: 87.6 us -> 65.8 us  [the longest x1 65.8 us: on_device(): lax.psum((embed_grad, bias_grad, gain_contribution, table_grad), 'row')]
    reduce_scatter x1, waiting for transfers between devices: 24.7 us -> 6.67 us  [on_device(): lax.psum_scatter(partial_rows, ('col', 'dp'), scatter_dimension=1, tiled=...]
    all_gather x1, waiting for transfers between devices: 45.2 us -> 31.7 us  [on_device(): qkv_rowwise = lax.all_gather(qkv_weight, 'row', axis=0, tiled=True)]
    ppermute x6, waiting for transfers between devices: 15.7 us -> 25.1 us  [from_behind(): return lax.ppermute(value, axis, pairs)]
    psum x1 -> x2, blocking collectives: 40.2 us -> 48.7 us  [the longest x1 35.3 us: on_device(): lax.psum((embed_grad, bias_grad, gain_contribution, table_grad), 'row')]
  transfers between devices with their start and end apart: 12 -> 13, of which waited for: 8 -> 9; matrix products, arithmetic and copies ran while one was open for 19% -> 6% of each run, Pallas kernels for 0% -> 0%
where the time goes in v1:
time: 414 us; the launch traced here: 413 us
  waiting for transfers between devices  256 us (62%)
  blocking collectives  62.1 us (15%)
  matrix products  32.4 us (8%)
  local copies, waits for them, and re-layouts  26.7 us (6%)
  between operations  22.4 us (5%)
  other arithmetic  7.36 us (2%)
  starting transfers between devices  6.07 us (1%)
    reduce_scatter x1, waiting for transfers between devices, on_device(): lax.psum_scatter(lax.dot_general(attended, cot_flat, (((0,), (0,)), ((),...  76.8 us
    psum x1, waiting for transfers between devices, on_device(): lax.psum((embed_grad, bias_grad, gain_contribution, table_grad), 'row')  65.8 us
    psum x1, blocking collectives, on_device(): lax.psum((embed_grad, bias_grad, gain_contribution, table_grad), 'row')  35.3 us
    all_gather x1, waiting for transfers between devices, on_device(): qkv_rowwise = lax.all_gather(qkv_weight, 'row', axis=0, tiled=True)  31.7 us
    all_gather x1, waiting for transfers between devices, on_device(): lax.all_gather(qkv_rowwise, ('col', 'dp'), axis=1, tiled=True)  31.3 us
    ppermute x6, waiting for transfers between devices, from_behind(): return lax.ppermute(value, axis, pairs)  25.1 us
    all_gather x1, waiting for transfers between devices, on_device(): lax.all_gather(out_columns, 'row', axis=0, tiled=True)  17.7 us
    all_gather x1, blocking collectives, on_device(): lax.all_gather(out_weight, ('col', 'dp'), axis=1, tiled=True)  13.4 us
  transfers between devices with their start and end apart: 13, of which 9 were waited for; matrix products, arithmetic and copies ran while one was open for 6% of the time, Pallas kernels for 0%

profile of v1, /device:TPU:0, one launch (start us, length us, event | category | flops | bytes accessed | tf_op | source)
XLA Modules:
  0.0 412.8 jit_solution(13182960756329515878)
XLA Ops:
  8.0 13.4 %all_gather.14 = bf16[96,1024]{1,0:T(8,128)(2,1)} all-gather(bf16[96,256]{1,0:T(8,128)(2,1)} %param.16), channel_id=1, replica_groups=mesh['row'=8,'col'=2,'dp'=2] {'col','dp'}, dimensions={1}, use_global_device_ids=true | all-gather | bytes 245760 | tf_op jit(solution)/shard_map/all_gather | solution.py:187
  21.5 31.7 %all-gather.4.cloned.1.call-done = bf16[1024,576]{0,1:T(8,128)(2,1)} async-done(((bf16[128,576]{0,1:T(8,128)(2,1)}), bf16[1024,576]{0,1:T(8,128)(2,1)}) %all-gather.4.cloned.1.call-update) | async-done | bytes 1179664 | tf_op jit(solution)/shard_map/all_gather | solution.py:184
  53.2 2.1 collective-permute-start.2
  63.4 2.6 convolution_bitcast_fusion
  66.0 16.5 %collective-permute-done = bf16[1,8,32,1024]{3,2,1,0:T(8,128)(2,1)S(1)} collective-permute-done((bf16[1,8,32,1024]{3,2,1,0:T(8,128)(2,1)S(1)}, bf16[1,8,32,1024]{3,2,1,0:T(8,128)(2,1)S(1)}, u32[]{:S(2)}, u32[]{:S(2)}) %collective-permute-start) | collective-permute-done | bytes 524320 | tf_op jit(solution)/shard_map/ppermute | solution.py:14
  89.8 17.7 %all-gather.8.cloned.1.call-done = bf16[768,1024]{1,0:T(8,128)(2,1)} async-done(((bf16[96,1024]{1,0:T(8,128)(2,1)}), bf16[768,1024]{1,0:T(8,128)(2,1)}) %all-gather.8.cloned.1.call-update) | async-done | bytes 1572880 | tf_op jit(solution)/shard_map/all_gather | solution.py:218
  107.5 2.8 convolution_convert_fusion.3
  113.5 31.3 %all-gather.6.cloned.1.call-done = bf16[1024,2304]{0,1:T(8,128)(2,1)} async-done(((bf16[1024,576]{0,1:T(8,128)(2,1)}), bf16[1024,2304]{0,1:T(8,128)(2,1)}) %all-gather.6.cloned.1.call-update) | async-done | bytes 4718608 | tf_op jit(solution)/shard_map/all_gather | solution.py:186
  144.9 3.8 convolution_convert_fusion
  151.1 2.6 reshape.366
  155.3 1.8 copy.178
  160.2 3.6 fusion.8
  163.8 2.6 multiply_reduce_fusion
  170.6 1.8 copy.177
  176.5 4.2 %multiply_reduce_fusion.1 = (f32[1024]{0:T(1024)S(1)}, f32[256]{0:T(256)S(1)}, f32[256]{0:T(256)S(1)}, f32[256,1024]{1,0:T(8,128)S(1)}) fusion(f32[1,4,8,8,1024]{4,3,2,1,0:T(8,128)S(1)} %copy.156, f32[256]{0:T(256)S(1)} %rsqrt.12, f32[256]{0:T(256)S(1)} %div.23, f32[1024]{0:T(1024)S(1)} %copy-done.16, bf16[1024,2304]{0,1:T(8,128)(2,1)} %all-gather.6.cloned.1.call-done, ...), kind=kOutput, calls=%fused_computation.41 | convolution fusion | flops 1213594112 | bytes 8007680 | tf_op jit(solution)/shard_map/dot_general | solution.py:153
  186.2 3.5 fusion.7
  189.7 1.8 copy.168
  191.9 8.1 %collective-permute-done.5 = bf16[1,8,32,1024]{3,2,1,0:T(8,128)(2,1)} collective-permute-done((bf16[1,8,32,1024]{3,2,1,0:T(8,128)(2,1)S(1)}, bf16[1,8,32,1024]{3,2,1,0:T(8,128)(2,1)}, u32[]{:S(2)}, u32[]{:S(2)}) %collective-permute-start.5) | collective-permute-done | bytes 524320 | tf_op jit(solution)/shard_map/ppermute | solution.py:14
  202.2 2.2 fusion.46
  204.5 65.8 %all-reduce.7.cloned.1.call-done = f32[48,1024]{1,0:T(8,128)} async-done(((f32[48,1024]{1,0:T(8,128)}), f32[48,1024]{1,0:T(8,128)}) %all-reduce.7.cloned.1.call-update) | async-done | bytes 196624 | tf_op jit(solution)/shard_map/psum | solution.py:255
  270.3 76.8 %reduce-scatter.3.cloned.1.call-done = f32[96,1024]{1,0:T(8,128)} async-done(((f32[768,1024]{1,0:T(8,128)}), f32[96,1024]{1,0:T(8,128)}) %reduce-scatter.3.cloned.1.call-update) | async-done | bytes 393232 | tf_op jit(solution)/shard_map/reduce_scatter | solution.py:222
  349.0 35.3 %all-reduce.2 = (f32[1024]{0:T(1024)S(1)}, f32[1024]{0:T(1024)S(1)}, f32[12,225]{1,0:T(8,128)S(1)}) all-reduce(f32[1024]{0:T(1024)S(1)} %add.142, f32[1024]{0:T(1024)S(1)} %get-tuple-element.71, f32[12,225]{1,0:T(8,128)S(1)} %fusion.1), channel_id=1, replica_groups=mesh['row'=8,'col'=2,'dp'=2] {'row'}, use_global_device_ids=true, to_apply=%region_13.14 | all-reduce | flops 4748 | bytes 37984 | tf_op jit(solution)/shard_map/psum | solution.py:255
  384.3 13.4 %all-reduce.3 = (f32[1024]{0:T(1024)}, f32[1024]{0:T(1024)}, f32[12,225]{1,0:T(8,128)}) all-reduce(f32[1024]{0:T(1024)S(1)} %get-tuple-element.74, f32[1024]{0:T(1024)S(1)} %get-tuple-element.75, f32[12,225]{1,0:T(8,128)S(1)} %get-tuple-element.76), channel_id=1, replica_groups=mesh['row'=8,'col'=2,'dp'=2] {'col','dp'}, use_global_device_ids=true, to_apply=%region_14.15 | all-reduce | flops 4748 | bytes 37984 | tf_op jit(solution)/shard_map/psum | solution.py:254
  397.7 6.7 %reduce-scatter.5.cloned.1.call-done = f32[96,256]{1,0:T(8,128)} async-done(((f32[96,1024]{1,0:T(8,128)}), f32[96,256]{1,0:T(8,128)}) %reduce-scatter.5.cloned.1.call-update) | async-done | bytes 98320 | tf_op jit(solution)/shard_map/reduce_scatter | solution.py:230
  (127 shorter events, 38.6 us)
Async XLA Ops:
  7.2 50.6 %copy-start = (bf16[48,1024]{1,0:T(8,128)(2,1)S(1)}, bf16[48,1024]{1,0:T(8,128)(2,1)}, u32[]{:S(2)}) copy-start(bf16[48,1024]{1,0:T(8,128)(2,1)} %param.12) | copy-start | bytes 294916
  7.2 46.0 %copy-start.3 = (bf16[1,8,32,1024]{3,2,1,0:T(8,128)(2,1)S(1)}, bf16[1,8,32,1024]{3,2,1,0:T(8,128)(2,1)}, u32[]{:S(2)}) copy-start(bf16[1,8,32,1024]{3,2,1,0:T(8,128)(2,1)} %param.11) | copy-start | bytes 1572868
  7.2 48.2 %copy-start.15 = (bf16[1,3,32,128]{3,2,1,0:T(8,128)(2,1)S(1)}, bf16[1,3,32,128]{3,2,1,0:T(8,128)(2,1)}, u32[]{:S(2)}) copy-start(bf16[1,3,32,128]{3,2,1,0:T(8,128)(2,1)} %param.10) | copy-start | bytes 73732
  7.2 45.9 %all-gather.4.cloned.1.call-start = ((), (), s32[]{:S(2)}) async-start(), calls=%async_computation.2 | async-start | bytes 1327104 | tf_op jit(solution)/shard_map/all_gather | solution.py:184
  7.9 99.5 %all-gather.8.cloned.1.call-start = ((), (), s32[]{:S(2)}) async-start(), calls=%async_computation.6 | async-start | bytes 1769472 | tf_op jit(solution)/shard_map/all_gather | solution.py:218
  21.4 36.4 %copy-start.19 = (f32[1024]{0:T(1024)S(1)}, f32[1024]{0:T(1024)}, u32[]{:S(2)}) copy-start(f32[1024]{0:T(1024)} %param.13) | copy-start | bytes 12292
  21.4 123.4 %all-gather.6.cloned.1.call-start = ((), (), s32[]{:S(2)}) async-start(), calls=%async_computation.3 | async-start | bytes 5898240 | tf_op jit(solution)/shard_map/all_gather | solution.py:186
  53.2 217.1 %all-reduce.7.cloned.1.call-start = ((), (), s32[]{:S(2)}) async-start(), calls=%async_computation.7 | async-start | bytes 393216 | tf_op jit(solution)/shard_map/psum | solution.py:255
  53.2 32.7 %collective-permute-start.2 = (bf16[1,8,32,1024]{3,2,1,0:T(8,128)(2,1)S(1)}, bf16[1,8,32,1024]{3,2,1,0:T(8,128)(2,1)S(1)}, u32[]{:S(2)}, u32[]{:S(2)}) collective-permute-start(bf16[1,8,32,1024]{3,2,1,0:T(8,128)(2,1)S(1)} %copy-done.3), channel_id=1, source_target_pairs={{0,28},{4,0},{8,4},{12,8},{16,12},{20,16},{24,20},{28,24},{1,29},{... | collective-permute-start | bytes 1572872 | tf_op jit(solution)/shard_map/ppermute | solution.py:14
  57.8 24.9 %copy-start.10 = (bf16[1,8,32,3,4,4]{2,1,5,4,3,0:T(8,128)(2,1)}, bf16[1,8,32,3,4,4]{2,1,5,4,3,0:T(8,128)(2,1)S(1)}, u32[]{:S(2)}) copy-start(bf16[1,8,32,3,4,4]{2,1,5,4,3,0:T(8,128)(2,1)S(1)} %copy.154) | copy-start | bytes 73732
  58.1 24.4 %collective-permute-start = (bf16[1,8,32,1024]{3,2,1,0:T(8,128)(2,1)S(1)}, bf16[1,8,32,1024]{3,2,1,0:T(8,128)(2,1)S(1)}, u32[]{:S(2)}, u32[]{:S(2)}) collective-permute-start(bf16[1,8,32,1024]{3,2,1,0:T(8,128)(2,1)S(1)} %fusion.11), channel_id=1, source_target_pairs={{0,28},{4,0},{8,4},{12,8},{16,12},{20,16},{24,20},{28,24},{1,29},{... | collective-permute-start | bytes 1572872 | tf_op jit(solution)/shard_map/ppermute | solution.py:14
  62.7 20.0 %copy-start.17 = (s32[4096]{0:T(1024)}, s32[4096]{0:T(1024)S(1)}, u32[]{:S(2)}) copy-start(s32[4096]{0:T(1024)S(1)} %eq.39) | copy-start | bytes 49156
  82.7 4.0 collective-permute-start.1
  86.2 1.5 collective-permute-start.3
  88.1 19.4 %copy-start.5 = (bf16[1,4,8,8,1024]{4,3,2,1,0:T(8,128)(2,1)}, bf16[1,4,8,8,1024]{4,3,2,1,0:T(8,128)(2,1)S(1)}, u32[]{:S(2)}) copy-start(bf16[1,4,8,8,1024]{4,3,2,1,0:T(8,128)(2,1)S(1)} %copy.169) | copy-start | bytes 1572868
  110.2 34.6 %copy-start.13 = (bf16[256,1024]{1,0:T(8,128)(2,1)S(1)}, bf16[256,1024]{1,0:T(8,128)(2,1)}, u32[]{:S(2)}) copy-start(bf16[256,1024]{1,0:T(8,128)(2,1)} %multiply_convert_fusion.3) | copy-start | bytes 1572868
  181.2 1.6 collective-permute-start.4
  183.0 17.0 %collective-permute-start.5 = (bf16[1,8,32,1024]{3,2,1,0:T(8,128)(2,1)S(1)}, bf16[1,8,32,1024]{3,2,1,0:T(8,128)(2,1)}, u32[]{:S(2)}, u32[]{:S(2)}) collective-permute-start(bf16[1,8,32,1024]{3,2,1,0:T(8,128)(2,1)S(1)} %fusion.25), channel_id=1, source_target_pairs={{0,4},{4,8},{8,12},{12,16},{16,20},{20,24},{24,28},{28,0},{1,5},{5... | collective-permute-start | bytes 1572872 | tf_op jit(solution)/shard_map/ppermute | solution.py:14
  191.9 10.3 %copy-start.6 = (bf16[1,4,8,8,1024]{4,3,2,1,0:T(8,128)(2,1)S(1)}, bf16[1,4,8,8,1024]{4,3,2,1,0:T(8,128)(2,1)}, u32[]{:S(2)}) copy-start(bf16[1,4,8,8,1024]{4,3,2,1,0:T(8,128)(2,1)} %copy-done.5) | copy-start | bytes 1572868
  202.1 145.0 %reduce-scatter.3.cloned.1.call-start = ((), (), s32[]{:S(2)}) async-start(), calls=%async_computation.4 | async-start | bytes 3538944 | tf_op jit(solution)/shard_map/reduce_scatter | solution.py:222
  204.4 142.8 %copy-start.7 = (f32[12,64,64]{1,2,0:T(8,128)S(1)}, f32[12,64,64]{1,2,0:T(8,128)}, u32[]{:S(2)}) copy-start(f32[12,64,64]{1,2,0:T(8,128)} %get-tuple-element.84) | copy-start | bytes 589828
  204.4 143.1 %copy-start.18 = (s32[4096]{0:T(1024)S(1)}, s32[4096]{0:T(1024)}, u32[]{:S(2)}) copy-start(s32[4096]{0:T(1024)} %copy-done.17) | copy-start | bytes 49156
  204.4 193.2 %all-reduce.9.cloned.1.call-start = ((), (), s32[]{:S(2)}) async-start(), calls=%async_computation.8 | async-start | bytes 393216 | tf_op jit(solution)/shard_map/psum | solution.py:254
  270.3 134.1 %reduce-scatter.5.cloned.1.call-start = ((), (), s32[]{:S(2)}) async-start(), calls=%async_computation.5 | async-start | bytes 491520 | tf_op jit(solution)/shard_map/reduce_scatter | solution.py:230
  (11 other events, 46.8 us)
Sparse Core Ops, SparseCore 0:
  10.1 43.0 all-gather.3
  55.3 52.0 all-gather.7
  109.0 35.7 all-gather.5
  202.2 67.9 all-reduce.6
  273.7 73.3 reduce-scatter.2
  349.3 31.1 all-reduce.8
  383.5 20.8 reduce-scatter.4
